TPU v7x, 32 devices: a whole 2x2x4 slice. The times are simulated.
32 devices in a mesh: seq: 8 (over z, core), fsdp: 4 (over y, x).
Axes of the slice: x: 2, y: 2, z: 4, core: 2. Of those that a mesh axis runs over, the one named last changes fastest.
Arguments:
- block_input: bfloat16 [8, 1472, 1152], P('fsdp', 'seq')
- key_mask: int32 [16, 736], P('fsdp'), may hold values from 0 to 1, as said below
- slot_flags: int32 [16], P('fsdp'), may hold values from 0 to 1, as said below
- norm1_gain: bfloat16 [1152], P('fsdp'), may hold values from 0.5 to 1.5
- norm1_bias: bfloat16 [1152], P('fsdp'), may hold values from -3 to 3
- qkv_weight: bfloat16 [1152, 3456], P('fsdp'), may hold values from -0.25 to 0.25
- query_bias: bfloat16 [1152], P('fsdp'), may hold values from -3 to 3
- value_bias: bfloat16 [1152], P('fsdp'), may hold values from -3 to 3
- proj_weight: bfloat16 [1152, 1152], P('fsdp'), may hold values from -0.375 to 0.375
- proj_bias: bfloat16 [1152], P('fsdp'), may hold values from -3 to 3
- norm2_gain: bfloat16 [1152], P('fsdp'), may hold values from 0.5 to 1.5
- norm2_bias: bfloat16 [1152], P('fsdp'), may hold values from -3 to 3
- up_weight: bfloat16 [1152, 4304], P('fsdp'), may hold values from -0.1875 to 0.1875
- up_bias: bfloat16 [4304], P('fsdp'), may hold values from -3 to 3
- down_weight: bfloat16 [4304, 1152], P(None, 'fsdp'), may hold values from -0.09375 to 0.09375
- down_bias: bfloat16 [1152], P('fsdp'), may hold values from -3 to 3
- out_grad: bfloat16 [8, 1472, 1152], P('fsdp', 'seq'), may hold values from -6 to 6
Outputs:
- block_output: bfloat16 [8, 1472, 1152], P('fsdp', 'seq')
- input_grad: float32 [8, 1472, 1152], P('fsdp', 'seq')
- norm1_gain_grad: float32 [1152], P('fsdp')
- norm1_bias_grad: float32 [1152], P('fsdp')
- qkv_weight_grad: float32 [1152, 3456], P('fsdp')
- query_bias_grad: float32 [1152], P('fsdp')
- value_bias_grad: float32 [1152], P('fsdp')
- proj_weight_grad: float32 [1152, 1152], P('fsdp')
- proj_bias_grad: float32 [1152], P('fsdp')
- norm2_gain_grad: float32 [1152], P('fsdp')
- norm2_bias_grad: float32 [1152], P('fsdp')
- up_weight_grad: float32 [1152, 4304], P('fsdp')
- up_bias_grad: float32 [4304], P('fsdp')
- down_weight_grad: float32 [4304, 1152], P(None, 'fsdp')
- down_bias_grad: float32 [1152], P('fsdp')
Inputs may be any that keep to these rules, and one draw needn't show every extreme that they name: `key_mask`: positions 729 and beyond are 0 in every slot; every position of a slot whose flag is 0 is 0. `slot_flags`: exactly max(1, 1) slots have flag 0, at places drawn from the seed.
All inputs are finite; a program needn't handle non-finite values.
Results may differ from a plain program's by a relative error of at most 0.012.
The roundings to bfloat16 on the way count: a program that leaves them out, or rounds other values in their place, can miss the bound.
Values may be sent and summed in bfloat16 or wider, within the bound.
A program may use at most 256 MiB of HBM per device.

v0:
```python
import jax
import jax.numpy as jnp
from jax import lax
from jax.sharding import PartitionSpec as P

HEAD = 72
epsilon = 1e-06


def as_sent(array):
    return jax.tree.map(lambda a: a.astype(jnp.bfloat16) if a.dtype == jnp.float32 else a, array)


def layer_norm(values, gain_vec, bias_vec):
    row_mean = jnp.mean(values, axis=-1, keepdims=True)
    centered = values - row_mean
    variance = jnp.mean(centered * centered, axis=-1, keepdims=True)
    return centered * lax.rsqrt(variance + epsilon) * gain_vec + bias_vec


def gelu_tanh(values):
    return (
        0.5
        * values
        * (1.0 + jnp.tanh(0.7978845608028654 * (values + 0.044715 * values * values * values)))
    )


def masked_scores(queries, key_vecs, key_live):
    score_scale = queries.shape[-1] ** (-0.5)
    scores = (
        jnp.einsum("qhd,khd->hqk", queries, key_vecs, preferred_element_type=jnp.float32)
        * score_scale
    )
    return scores + ((key_live.astype(jnp.float32) - 1.0) * 10000.0)[None, None, :]


def attend_forward(packed):
    queries, key_vecs, value_vecs, key_live = packed
    shifted = masked_scores(queries, key_vecs, key_live)
    row_max = jnp.max(shifted, axis=-1, keepdims=True)
    exp_terms = jnp.exp(shifted - row_max)
    row_total = jnp.sum(exp_terms, axis=-1, keepdims=True)
    weights_low = (exp_terms / row_total).astype(jnp.bfloat16)
    attended = jnp.einsum(
        "hqk,khd->qhd", weights_low, value_vecs, preferred_element_type=jnp.float32
    )
    return (attended.astype(jnp.bfloat16), row_max + jnp.log(row_total))


def attend_backward(packed):
    queries, key_vecs, value_vecs, key_live, log_total, grad_out = packed
    score_scale = queries.shape[-1] ** (-0.5)
    shifted = masked_scores(queries, key_vecs, key_live)
    probabilities = jnp.exp(shifted - log_total)
    weights_low = probabilities.astype(jnp.bfloat16)
    grad_probs = jnp.einsum(
        "qhd,khd->hqk", grad_out, value_vecs, preferred_element_type=jnp.float32
    )
    row_dot = jnp.sum(probabilities * grad_probs, axis=-1, keepdims=True)
    grad_scores = (probabilities * (grad_probs - row_dot)).astype(jnp.bfloat16)
    grad_q = (
        jnp.einsum("hqk,khd->qhd", grad_scores, key_vecs, preferred_element_type=jnp.float32)
        * score_scale
    ).astype(jnp.bfloat16)
    grad_k = (
        jnp.einsum("hqk,qhd->khd", grad_scores, queries, preferred_element_type=jnp.float32)
        * score_scale
    ).astype(jnp.bfloat16)
    grad_v = jnp.einsum(
        "hqk,qhd->khd", weights_low, grad_out, preferred_element_type=jnp.float32
    ).astype(jnp.bfloat16)
    return (grad_q, grad_k, grad_v)


def forward_pass(block_input, key_mask, row_flags, gathered, repeat):
    (
        gain_one,
        bias_one,
        qkv_full,
        query_shift,
        value_shift,
        proj_full,
        proj_shift,
        gain_two,
        bias_two,
        up_full,
        up_shift,
        down_full,
        down_shift,
    ) = gathered
    pair_count, part_rows, model_width = block_input.shape
    token_rows = block_input.reshape(pair_count * part_rows, model_width).astype(jnp.float32)
    normed, norm_one_back = jax.vjp(
        layer_norm, token_rows, gain_one.astype(jnp.float32), bias_one.astype(jnp.float32)
    )
    normed_low = normed.astype(jnp.bfloat16)
    mixed_rows = jnp.dot(normed_low, qkv_full, preferred_element_type=jnp.float32)
    token_shape = (pair_count, part_rows, model_width)
    queries = (
        (mixed_rows[:, :model_width] + query_shift.astype(jnp.float32))
        .astype(jnp.bfloat16)
        .reshape(token_shape)
    )
    key_vecs = (
        mixed_rows[:, model_width : 2 * model_width].astype(jnp.bfloat16).reshape(token_shape)
    )
    value_vecs = (
        (mixed_rows[:, 2 * model_width :] + value_shift.astype(jnp.float32))
        .astype(jnp.bfloat16)
        .reshape(token_shape)
    )
    if repeat:
        head_parts = (
            lax.all_to_all(queries, "seq", split_axis=2, concat_axis=1, tiled=True),
            lax.all_to_all(key_vecs, "seq", split_axis=2, concat_axis=1, tiled=True),
            lax.all_to_all(value_vecs, "seq", split_axis=2, concat_axis=1, tiled=True),
        )
    else:
        head_parts = (
            lax.all_to_all(queries, "seq", split_axis=2, concat_axis=1, tiled=True),
            lax.all_to_all(key_vecs, "seq", split_axis=2, concat_axis=1, tiled=True),
            lax.all_to_all(value_vecs, "seq", split_axis=2, concat_axis=1, tiled=True),
        )
    layout = head_parts[0].shape
    head_shape = (pair_count * 2, layout[1] // 2, layout[2] // HEAD, HEAD)
    split_heads = (
        head_parts[0].reshape(head_shape),
        head_parts[1].reshape(head_shape),
        head_parts[2].reshape(head_shape),
    )
    attended, log_total = lax.map(attend_forward, split_heads + (key_mask,))
    attended = attended.reshape(layout)
    if repeat:
        merged = lax.all_to_all(attended, "seq", split_axis=1, concat_axis=2, tiled=True)
    else:
        merged = lax.all_to_all(attended, "seq", split_axis=1, concat_axis=2, tiled=True)
    merged_rows = merged.reshape(pair_count * part_rows, model_width)
    hidden = (
        token_rows
        + jnp.dot(merged_rows, proj_full, preferred_element_type=jnp.float32)
        + proj_shift.astype(jnp.float32)
    )
    second, norm_two_back = jax.vjp(
        layer_norm, hidden, gain_two.astype(jnp.float32), bias_two.astype(jnp.float32)
    )
    second_low = second.astype(jnp.bfloat16)
    gate_in = jnp.dot(second_low, up_full, preferred_element_type=jnp.float32) + up_shift.astype(
        jnp.float32
    )
    active, gelu_back = jax.vjp(gelu_tanh, gate_in)
    active_low = active.astype(jnp.bfloat16)
    result = (
        hidden
        + jnp.dot(active_low, down_full, preferred_element_type=jnp.float32)
        + down_shift.astype(jnp.float32)
    )
    output = (result.reshape(token_shape) * row_flags[:, None, None]).astype(jnp.bfloat16)
    return dict(
        normed_low=normed_low,
        norm_one_back=norm_one_back,
        split_heads=split_heads,
        log_total=log_total,
        merged_rows=merged_rows,
        norm_two_back=norm_two_back,
        second_low=second_low,
        gelu_back=gelu_back,
        active_low=active_low,
        output=output,
    )


def shards(
    block_input,
    key_mask,
    slot_flags,
    norm1_gain,
    norm1_bias,
    qkv_weight,
    query_bias,
    value_bias,
    proj_weight,
    proj_bias,
    norm2_gain,
    norm2_bias,
    up_weight,
    up_bias,
    down_weight,
    down_bias,
    out_grad,
):
    gathered = (
        lax.all_gather(norm1_gain, "fsdp", axis=0, tiled=True),
        lax.all_gather(norm1_bias, "fsdp", axis=0, tiled=True),
        lax.all_gather(qkv_weight, "fsdp", axis=0, tiled=True),
        lax.all_gather(query_bias, "fsdp", axis=0, tiled=True),
        lax.all_gather(value_bias, "fsdp", axis=0, tiled=True),
        lax.all_gather(proj_weight, "fsdp", axis=0, tiled=True),
        lax.all_gather(proj_bias, "fsdp", axis=0, tiled=True),
        lax.all_gather(norm2_gain, "fsdp", axis=0, tiled=True),
        lax.all_gather(norm2_bias, "fsdp", axis=0, tiled=True),
        lax.all_gather(up_weight, "fsdp", axis=0, tiled=True),
        lax.all_gather(up_bias, "fsdp", axis=0, tiled=True),
        lax.all_gather(down_weight, "fsdp", axis=1, tiled=True),
        lax.all_gather(down_bias, "fsdp", axis=0, tiled=True),
    )
    which_half = lax.axis_index("seq") // (lax.axis_size("seq") // 2)
    flag_pairs = slot_flags.astype(jnp.float32).reshape(-1, 2)
    row_flags = jnp.where(which_half == 0, flag_pairs[:, 0], flag_pairs[:, 1])
    first = forward_pass(block_input, key_mask, row_flags, gathered, False)
    kept_state = forward_pass(block_input, key_mask, row_flags, gathered, True)
    qkv_full = gathered[2]
    proj_full = gathered[5]
    up_full = gathered[9]
    down_full = gathered[11]
    pair_count, part_rows, model_width = block_input.shape
    grad_rows = (out_grad.astype(jnp.float32) * row_flags[:, None, None]).reshape(
        pair_count * part_rows, model_width
    )
    grad_low = grad_rows.astype(jnp.bfloat16)
    down_weight_grad = jnp.einsum(
        "rf,rd->fd", kept_state["active_low"], grad_low, preferred_element_type=jnp.float32
    )
    down_bias_grad = jnp.sum(grad_rows, axis=0)
    grad_active = jnp.einsum("rd,fd->rf", grad_low, down_full, preferred_element_type=jnp.float32)
    grad_gate = kept_state["gelu_back"](grad_active)[0].astype(jnp.bfloat16)
    up_weight_grad = jnp.einsum(
        "rd,rf->df", kept_state["second_low"], grad_gate, preferred_element_type=jnp.float32
    )
    up_bias_grad = jnp.sum(grad_gate.astype(jnp.float32), axis=0)
    grad_second = jnp.einsum("rf,df->rd", grad_gate, up_full, preferred_element_type=jnp.float32)
    grad_hidden_norm, norm2_gain_grad, norm2_bias_grad = kept_state["norm_two_back"](grad_second)
    grad_hidden = grad_rows + grad_hidden_norm
    grad_branch = grad_hidden.astype(jnp.bfloat16)
    proj_weight_grad = jnp.einsum(
        "ri,ro->io", kept_state["merged_rows"], grad_branch, preferred_element_type=jnp.float32
    )
    proj_bias_grad = jnp.sum(grad_branch.astype(jnp.float32), axis=0)
    grad_merged = jnp.einsum(
        "ro,io->ri", grad_branch, proj_full, preferred_element_type=jnp.float32
    ).astype(jnp.bfloat16)
    grad_heads = lax.all_to_all(
        grad_merged.reshape(pair_count, part_rows, model_width),
        "seq",
        split_axis=2,
        concat_axis=1,
        tiled=True,
    )
    split_heads = kept_state["split_heads"]
    head_shape = split_heads[0].shape
    grad_q, grad_k, grad_v = lax.map(
        attend_backward,
        split_heads + (key_mask, kept_state["log_total"], grad_heads.reshape(head_shape)),
    )
    layout = grad_heads.shape
    back_parts = (
        lax.all_to_all(
            as_sent(grad_q.reshape(layout)), "seq", split_axis=1, concat_axis=2, tiled=True
        ),
        lax.all_to_all(
            as_sent(grad_k.reshape(layout)), "seq", split_axis=1, concat_axis=2, tiled=True
        ),
        lax.all_to_all(
            as_sent(grad_v.reshape(layout)), "seq", split_axis=1, concat_axis=2, tiled=True
        ),
    )
    grad_mixed = jnp.concatenate(
        (
            back_parts[0].reshape(-1, model_width),
            back_parts[1].reshape(-1, model_width),
            back_parts[2].reshape(-1, model_width),
        ),
        axis=1,
    )
    qkv_weight_grad = jnp.einsum(
        "ri,ro->io", kept_state["normed_low"], grad_mixed, preferred_element_type=jnp.float32
    )
    query_bias_grad = jnp.sum(back_parts[0].astype(jnp.float32), axis=(0, 1))
    value_bias_grad = jnp.sum(back_parts[2].astype(jnp.float32), axis=(0, 1))
    grad_normed = jnp.einsum("ro,io->ri", grad_mixed, qkv_full, preferred_element_type=jnp.float32)
    grad_rows_norm, norm1_gain_grad, norm1_bias_grad = kept_state["norm_one_back"](grad_normed)
    input_grad = (grad_hidden + grad_rows_norm).reshape(pair_count, part_rows, model_width)
    shard_terms = (
        lax.psum_scatter(norm1_gain_grad, "fsdp", scatter_dimension=0, tiled=True),
        lax.psum_scatter(norm1_bias_grad, "fsdp", scatter_dimension=0, tiled=True),
        lax.psum_scatter(qkv_weight_grad, "fsdp", scatter_dimension=0, tiled=True),
        lax.psum_scatter(query_bias_grad, "fsdp", scatter_dimension=0, tiled=True),
        lax.psum_scatter(value_bias_grad, "fsdp", scatter_dimension=0, tiled=True),
        lax.psum_scatter(proj_weight_grad, "fsdp", scatter_dimension=0, tiled=True),
        lax.psum_scatter(proj_bias_grad, "fsdp", scatter_dimension=0, tiled=True),
        lax.psum_scatter(norm2_gain_grad, "fsdp", scatter_dimension=0, tiled=True),
        lax.psum_scatter(norm2_bias_grad, "fsdp", scatter_dimension=0, tiled=True),
        lax.psum_scatter(up_weight_grad, "fsdp", scatter_dimension=0, tiled=True),
        lax.psum_scatter(up_bias_grad, "fsdp", scatter_dimension=0, tiled=True),
        lax.psum_scatter(down_weight_grad, "fsdp", scatter_dimension=1, tiled=True),
        lax.psum_scatter(down_bias_grad, "fsdp", scatter_dimension=0, tiled=True),
    )
    summed = lax.psum(
        (
            shard_terms[0],
            shard_terms[1],
            shard_terms[2],
            shard_terms[3],
            shard_terms[4],
            shard_terms[5],
            shard_terms[6],
            shard_terms[7],
            shard_terms[8],
            shard_terms[9],
            shard_terms[10],
            shard_terms[11],
            shard_terms[12],
        ),
        "seq",
    )
    return (
        first["output"],
        input_grad,
        summed[0],
        summed[1],
        summed[2],
        summed[3],
        summed[4],
        summed[5],
        summed[6],
        summed[7],
        summed[8],
        summed[9],
        summed[10],
        summed[11],
        summed[12],
    )


def solution(mesh):
    in_specs = (
        P("fsdp", "seq", None),
        P("fsdp", None),
        P("fsdp"),
        P("fsdp"),
        P("fsdp"),
        P("fsdp", None),
        P("fsdp"),
        P("fsdp"),
        P("fsdp", None),
        P("fsdp"),
        P("fsdp"),
        P("fsdp"),
        P("fsdp", None),
        P("fsdp"),
        P(None, "fsdp"),
        P("fsdp"),
        P("fsdp", "seq", None),
    )
    out_specs = (
        P("fsdp", "seq", None),
        P("fsdp", "seq", None),
        P("fsdp"),
        P("fsdp"),
        P("fsdp", None),
        P("fsdp"),
        P("fsdp"),
        P("fsdp", None),
        P("fsdp"),
        P("fsdp"),
        P("fsdp"),
        P("fsdp", None),
        P("fsdp"),
        P(None, "fsdp"),
        P("fsdp"),
    )
    return jax.shard_map(shards, mesh=mesh, in_specs=in_specs, out_specs=out_specs, check_vma=False)
```

profile of v0, /device:TPU:0, one launch (start us, length us, event | category | flops | bytes accessed | tf_op | source)
XLA Modules:
  0.0 1495.3 jit_solution(833111917682874269)
XLA Ops:
  14.1 19.2 %all-reduce.21 = (bf16[1152]{0:T(1024)(128)(2,1)S(1)}, bf16[1152]{0:T(1024)(128)(2,1)S(1)}, bf16[1152]{0:T(1024)(128)(2,1)S(1)}, bf16[1152]{0:T(1024)(128)(2,1)S...) all-reduce(bf16[1152]{0:T(1024)(128)(2,1)S(1)} %dynamic-update-slic, ...), channel_id=1, replica_groups=mesh['seq'=8,'fsdp'=4] {'fsdp'}, use_global_device_ids=true, to_apply=%add.1 | all-reduce | flops 13520 | bytes 54080
  35.9 61.2 %all-gather.5.cloned.1.call-done = bf16[1152,3456]{1,0:T(8,128)(2,1)} async-done(((bf16[288,3456]{1,0:T(8,128)(2,1)}), bf16[1152,3456]{1,0:T(8,128)(2,1)}) %all-gather.5.cloned.1.call-update) | async-done | bytes 7962640 | tf_op jit(solution)/shard_map/all_gather | solution.py:195
  117.2 26.7 %all-to-all-done = bf16[2,184,1152]{1,0,2:T(2,128)(2,1)S(1)} async-done(((bf16[2,184,1152]{1,0,2:T(2,128)(2,1)}), bf16[2,184,1152]{1,0,2:T(2,128)(2,1)S(1)}, u32[]{:S(2)}, u32[]{:S(2)}) %all-to-all-start) | async-done | bytes 847904 | tf_op jit(solution)/shard_map/all_to_all | solution.py:123
  154.6 22.2 %all-to-all-done.1 = bf16[2,184,1152]{1,0,2:T(2,128)(2,1)S(1)} async-done(((bf16[2,184,1152]{1,0,2:T(2,128)(2,1)}), bf16[2,184,1152]{1,0,2:T(2,128)(2,1)S(1)}, u32[]{:S(2)}, u32[]{:S(2)}) %all-to-all-start.1) | async-done | bytes 847904 | tf_op jit(solution)/shard_map/all_to_all | solution.py:121
  191.9 18.5 %all-to-all-done.2 = bf16[2,184,1152]{1,0,2:T(2,128)(2,1)} async-done(((bf16[2,184,1152]{1,0,2:T(2,128)(2,1)}), bf16[2,184,1152]{1,0,2:T(2,128)(2,1)}, u32[]{:S(2)}, u32[]{:S(2)}) %all-to-all-start.2) | async-done | bytes 847904 | tf_op jit(solution)/shard_map/all_to_all | solution.py:122
  219.7 29.2 %while.42 = (s32[]{:T(128)}, bf16[4,736,2,72]{1,3,2,0:T(8,128)(2,1)}, bf16[4,736,2,72]{1,3,2,0:T(8,128)(2,1)}, bf16[4,736,2,72]{1,3,2,0:T(8,128)(2,1)S(1)}, bf16...) while((s32[]{:T(128)}, bf16[4,736,2,72]{1,3,2,0:T(8,128)(2,1)}, ...), condition=%wide.region_5.6_spmd, body=%wide.region_2.5_spmd.sunk | while | flops 318626176 | bytes 9764185 | solution.py:132
  267.1 19.5 %while.43 = (s32[]{:T(128)}, bf16[4,736,2,72]{1,3,2,0:T(8,128)(2,1)}, f32[4,2,736,1]{2,1,3,0:T(2,128)S(1)}, bf16[4,736,2,72]{1,3,2,0:T(8,128)(2,1)}, bf16[4,736,...) while((s32[]{:T(128)}, ...), condition=%wide.region_11.12_spmd, body=%wide.region_8.11_spmd.sunk | while | flops 325124320 | bytes 13951333 | solution.py:132
  317.1 26.0 %all-to-all-done.4 = bf16[2,1472,144]{2,0,1:T(2,128)(2,1)} async-done(((bf16[2,1472,144]{2,0,1:T(2,128)(2,1)}), bf16[2,1472,144]{2,0,1:T(2,128)(2,1)}, u32[]{:S(2)}, u32[]{:S(2)}) %all-to-all-start.4) | async-done | bytes 847904 | tf_op jit(solution)/shard_map/all_to_all | solution.py:135
  362.3 17.5 %fusion.111 = f32[368,1152]{1,0:T(8,128)} fusion(f32[368,1152]{1,0:T(8,128)} %copy-done.22, bf16[4304,1152]{0,1:T(8,128)(2,1)} %all-gather.11.cloned.1.call-done, bf16[1152,4304]{1,0:T(8,128)(2,1)} %all-gather.9.cloned.1.call-done, f32[4304]{0:T(1024)S(1)} %convert_element_type.223, f32[1152]{0:T(1024)S(1)} %convert_element_type.225, ...), kind=kOutput, calls=%fused_computation.119 | convolution fusion | flops 7317288448 | bytes 23258304 | tf_op jit(solution)/shard_map/dot_general | solution.py:155
  392.0 9.9 convert_reduce_fusion
  431.7 23.5 %all-to-all-done.5 = bf16[2,184,1152]{1,0,2:T(2,128)(2,1)} async-done(((bf16[2,184,1152]{1,0,2:T(2,128)(2,1)}), bf16[2,184,1152]{1,0,2:T(2,128)(2,1)}, u32[]{:S(2)}, u32[]{:S(2)}) %all-to-all-start.5) | async-done | bytes 847904 | tf_op jit(solution)/shard_map/all_to_all | solution.py:242
  467.2 37.2 %while.44 = (s32[]{:T(128)}, bf16[4,736,2,72]{1,3,2,0:T(8,128)(2,1)}, bf16[4,736,2,72]{1,3,2,0:T(8,128)(2,1)}, bf16[4,736,2,72]{1,3,2,0:T(8,128)(2,1)}, bf16[4,7...) while((s32[]{:T(128)}, ...), condition=%wide.region_18.19_spmd, body=%wide.region_16.18_spmd.sunk | while | flops 796823808 | bytes 38734360 | solution.py:251
  527.0 24.1 %all-to-all-done.6 = bf16[2,1472,144]{2,0,1:T(2,128)(2,1)S(1)} async-done(((bf16[2,1472,144]{2,0,1:T(2,128)(2,1)}), bf16[2,1472,144]{2,0,1:T(2,128)(2,1)S(1)}, u32[]{:S(2)}, u32[]{:S(2)}) %all-to-all-start.6) | async-done | bytes 847904 | tf_op jit(solution)/shard_map/all_to_all | solution.py:257
  567.7 24.2 %all-to-all-done.7 = bf16[2,1472,144]{2,0,1:T(2,128)(2,1)} async-done(((bf16[2,1472,144]{2,0,1:T(2,128)(2,1)}), bf16[2,1472,144]{2,0,1:T(2,128)(2,1)}, u32[]{:S(2)}, u32[]{:S(2)}) %all-to-all-start.7) | async-done | bytes 847904 | tf_op jit(solution)/shard_map/all_to_all | solution.py:260
  614.3 18.2 %all-to-all-done.8 = bf16[2,1472,144]{2,0,1:T(2,128)(2,1)} async-done(((bf16[2,1472,144]{2,0,1:T(2,128)(2,1)}), bf16[2,1472,144]{2,0,1:T(2,128)(2,1)}, u32[]{:S(2)}, u32[]{:S(2)}) %all-to-all-start.8) | async-done | bytes 847904 | tf_op jit(solution)/shard_map/all_to_all | solution.py:263
  656.2 11.5 fusion.133
  668.8 13.5 fusion.104
  682.4 117.7 %reduce-scatter.5.cloned.1.call-done = f32[288,3456]{1,0:T(8,128)} async-done(((f32[1152,3456]{1,0:T(8,128)}), f32[288,3456]{1,0:T(8,128)}) %reduce-scatter.5.cloned.1.call-update) | async-done | bytes 3981328 | tf_op jit(solution)/shard_map/reduce_scatter | solution.py:286
  800.2 183.5 %reduce-scatter.9.cloned.1.call-done = f32[288,4304]{1,0:T(8,128)} async-done(((f32[1152,4304]{1,0:T(8,128)}), f32[288,4304]{1,0:T(8,128)}) %reduce-scatter.9.cloned.1.call-update) | async-done | bytes 4958224 | tf_op jit(solution)/shard_map/reduce_scatter | solution.py:293
  983.6 183.5 %reduce-scatter.11.cloned.1.call-done = f32[4304,288]{0,1:T(8,128)} async-done(((f32[4304,1152]{0,1:T(8,128)}), f32[4304,288]{0,1:T(8,128)}) %reduce-scatter.11.cloned.1.call-update) | async-done | bytes 4958224 | tf_op jit(solution)/shard_map/reduce_scatter | solution.py:295
  1174.8 10.6 fusion.134
  1185.4 17.2 %all-reduce.20 = (f32[1152]{0:T(1024)S(1)}, f32[1152]{0:T(1024)S(1)}, f32[1152]{0:T(1024)S(1)}, f32[1152]{0:T(1024)S(1)}, f32[1152]{0:T(1024)S(1)}, /*index=5*/f...) all-reduce(f32[1152]{0:T(1024)S(1)} %get-tuple-element.412, ...), channel_id=2, replica_groups=mesh['seq'=8,'fsdp'=4] {'fsdp'}, use_global_device_ids=true, to_apply=%region_22.23.clone | all-reduce | flops 13520 | bytes 108160
  1208.4 28.3 %all-reduce.18 = (f32[288]{0:T(512)}, f32[288]{0:T(512)}, f32[288]{0:T(512)}, f32[288]{0:T(512)}, f32[288]{0:T(512)}, /*index=5*/f32[288]{0:T(512)}, f32[288]{0:T(512)}, f32[1076]{0:T(1024)}, f32[288]{0:T(512)}) all-reduce(f32[288]{0:T(512)S(1)} %dynamic-slice.10, ...), channel_id=1, replica_groups=mesh['seq'=8,'fsdp'=4] {'seq'}, use_global_device_ids=true, to_apply=%region_23.24 | all-reduce | flops 3380 | bytes 27040 | tf_op jit(solution)/shard_map/psum | solution.py:298
  1239.8 237.1 %all-reduce.24.cloned.1.call-done = (f32[288,3456]{1,0:T(8,128)}, f32[288,1152]{1,0:T(8,128)}, f32[288,4304]{1,0:T(8,128)}, f32[4304,288]{0,1:T(8,128)}) async-done(((f32[288,3456]{1,0:T(8,128)}, f32[288,1152]{1,0:T(8,128)}, f32[288,4304]{1,0:T(8,128)}, f32[4304,288]{0,1:T(8,128)}), (f32[288,3456]{1,0:T(8,128)}, f32[288,1152]{1,0:T(8,128)}, f32[288,4304]{1,0:T(8,128)}, ...) | async-done | bytes 15224848 | tf_op jit(solution)/shard_map/psum | solution.py:298
  (360 shorter events, 383.1 us)
Async XLA Ops:
  7.3 89.8 %all-gather.5.cloned.1.call-start = ((), (), s32[]{:S(2)}) async-start(), calls=%async_computation.13 | async-start | bytes 9953280 | tf_op jit(solution)/shard_map/all_gather | solution.py:195
  8.0 345.4 %all-gather.7.cloned.1.call-start = ((), (), s32[]{:S(2)}) async-start(), calls=%async_computation.14 | async-start | bytes 3317760 | tf_op jit(solution)/shard_map/all_gather | solution.py:198
  8.8 353.5 %all-gather.11.cloned.1.call-start = ((), (), s32[]{:S(2)}) async-start(), calls=%async_computation.16 | async-start | bytes 12533760 | tf_op jit(solution)/shard_map/all_gather | solution.py:204
  11.7 91.4 %copy-start.34 = (f32[368]{0:T(512)}, f32[368]{0:T(512)S(1)}, u32[]{:S(2)}) copy-start(f32[368]{0:T(512)S(1)} %div.83) | copy-start | bytes 4420
  33.3 69.9 %copy-start.25 = (f32[1152]{0:T(1024)}, f32[1152]{0:T(1024)S(1)}, u32[]{:S(2)}) copy-start(f32[1152]{0:T(1024)S(1)} %convert_element_type.212) | copy-start | bytes 13828
  35.9 67.2 %copy-start.14 = (bf16[368,1152]{1,0:T(8,128)(2,1)}, bf16[368,1152]{1,0:T(8,128)(2,1)S(1)}, u32[]{:S(2)}) copy-start(bf16[368,1152]{1,0:T(8,128)(2,1)S(1)} %get-tuple-element.505) | copy-start | bytes 2543620
  110.0 33.9 %all-to-all-start = ((bf16[2,184,1152]{1,0,2:T(2,128)(2,1)}), bf16[2,184,1152]{1,0,2:T(2,128)(2,1)S(1)}, u32[]{:S(2)}, u32[]{:S(2)}) async-start(bf16[2,184,1152]{1,0,2:T(2,128)(2,1)} %copy.166), calls=%async_computation | async-start | bytes 2359296 | tf_op jit(solution)/shard_map/all_to_all | solution.py:123
  143.9 32.9 %all-to-all-start.1 = ((bf16[2,184,1152]{1,0,2:T(2,128)(2,1)}), bf16[2,184,1152]{1,0,2:T(2,128)(2,1)S(1)}, u32[]{:S(2)}, u32[]{:S(2)}) async-start(bf16[2,184,1152]{1,0,2:T(2,128)(2,1)} %copy.169), calls=%async_computation.1 | async-start | bytes 2359296 | tf_op jit(solution)/shard_map/all_to_all | solution.py:121
  176.8 33.6 %all-to-all-start.2 = ((bf16[2,184,1152]{1,0,2:T(2,128)(2,1)}), bf16[2,184,1152]{1,0,2:T(2,128)(2,1)}, u32[]{:S(2)}, u32[]{:S(2)}) async-start(bf16[2,184,1152]{1,0,2:T(2,128)(2,1)} %copy.172), calls=%async_computation.2 | async-start | bytes 2359296 | tf_op jit(solution)/shard_map/all_to_all | solution.py:122
  181.1 181.2 %all-gather.9.cloned.1.call-start = ((), (), s32[]{:S(2)}) async-start(), calls=%async_computation.15 | async-start | bytes 12533760 | tf_op jit(solution)/shard_map/all_gather | solution.py:202
  261.3 41.1 %all-to-all-start.3 = ((bf16[2,1472,144]{2,0,1:T(2,128)(2,1)}), bf16[2,1472,144]{2,0,1:T(2,128)(2,1)}, u32[]{:S(2)}, u32[]{:S(2)}) async-start(bf16[2,1472,144]{2,0,1:T(2,128)(2,1)} %copy.179), calls=%async_computation.3 | async-start | bytes 3014656 | tf_op jit(solution)/shard_map/all_to_all | solution.py:137
  302.5 40.7 %all-to-all-start.4 = ((bf16[2,1472,144]{2,0,1:T(2,128)(2,1)}), bf16[2,1472,144]{2,0,1:T(2,128)(2,1)}, u32[]{:S(2)}, u32[]{:S(2)}) async-start(bf16[2,1472,144]{2,0,1:T(2,128)(2,1)} %copy.185), calls=%async_computation.4 | async-start | bytes 3014656 | tf_op jit(solution)/shard_map/all_to_all | solution.py:135
  421.5 33.6 %all-to-all-start.5 = ((bf16[2,184,1152]{1,0,2:T(2,128)(2,1)}), bf16[2,184,1152]{1,0,2:T(2,128)(2,1)}, u32[]{:S(2)}, u32[]{:S(2)}) async-start(bf16[2,184,1152]{1,0,2:T(2,128)(2,1)} %copy.187), calls=%async_computation.5 | async-start | bytes 2359296 | tf_op jit(solution)/shard_map/all_to_all | solution.py:242
  425.8 256.6 %reduce-scatter.7.cloned.1.call-start = ((), (), s32[]{:S(2)}) async-start(), calls=%async_computation.18 | async-start | bytes 6635520 | tf_op jit(solution)/shard_map/reduce_scatter | solution.py:289
  511.1 40.1 %all-to-all-start.6 = ((bf16[2,1472,144]{2,0,1:T(2,128)(2,1)}), bf16[2,1472,144]{2,0,1:T(2,128)(2,1)S(1)}, u32[]{:S(2)}, u32[]{:S(2)}) async-start(bf16[2,1472,144]{2,0,1:T(2,128)(2,1)} %copy.195), calls=%async_computation.6 | async-start | bytes 3014656 | tf_op jit(solution)/shard_map/all_to_all | solution.py:257
  551.1 40.7 %all-to-all-start.7 = ((bf16[2,1472,144]{2,0,1:T(2,128)(2,1)}), bf16[2,1472,144]{2,0,1:T(2,128)(2,1)}, u32[]{:S(2)}, u32[]{:S(2)}) async-start(bf16[2,1472,144]{2,0,1:T(2,128)(2,1)} %copy.198), calls=%async_computation.7 | async-start | bytes 3014656 | tf_op jit(solution)/shard_map/all_to_all | solution.py:260
  591.8 40.7 %all-to-all-start.8 = ((bf16[2,1472,144]{2,0,1:T(2,128)(2,1)}), bf16[2,1472,144]{2,0,1:T(2,128)(2,1)}, u32[]{:S(2)}, u32[]{:S(2)}) async-start(bf16[2,1472,144]{2,0,1:T(2,128)(2,1)} %copy.202), calls=%async_computation.8 | async-start | bytes 3014656 | tf_op jit(solution)/shard_map/all_to_all | solution.py:263
  596.1 204.0 %reduce-scatter.5.cloned.1.call-start = ((), (), s32[]{:S(2)}) async-start(), calls=%async_computation.17 | async-start | bytes 19906560 | tf_op jit(solution)/shard_map/reduce_scatter | solution.py:286
  654.8 328.9 %reduce-scatter.9.cloned.1.call-start = ((), (), s32[]{:S(2)}) async-start(), calls=%async_computation.19 | async-start | bytes 25067520 | tf_op jit(solution)/shard_map/reduce_scatter | solution.py:293
  667.7 499.4 %reduce-scatter.11.cloned.1.call-start = ((), (), s32[]{:S(2)}) async-start(), calls=%async_computation.20 | async-start | bytes 25067520 | tf_op jit(solution)/shard_map/reduce_scatter | solution.py:295
  682.4 794.5 %all-reduce.24.cloned.1.call-start = ((), (), s32[]{:S(2)}) async-start(), calls=%async_computation.21 | async-start | bytes 30670848 | tf_op jit(solution)/shard_map/psum | solution.py:298
  1174.8 28.5 %copy-start.33 = (f32[368]{0:T(512)S(1)}, f32[368]{0:T(512)}, u32[]{:S(2)}) copy-start(f32[368]{0:T(512)} %copy-done.32) | copy-start | bytes 4420
  1203.3 33.5 %copy-start.4 = (f32[368,1152]{1,0:T(8,128)S(1)}, f32[368,1152]{1,0:T(8,128)}, u32[]{:S(2)}) copy-start(f32[368,1152]{1,0:T(8,128)} %copy-done.3) | copy-start | bytes 5087236
  1203.3 33.5 %copy-start.29 = (f32[368]{0:T(512)S(1)}, f32[368]{0:T(512)}, u32[]{:S(2)}) copy-start(f32[368]{0:T(512)} %copy-done.28) | copy-start | bytes 4420
  (55 other events, 291.6 us)
Sparse Core Ops, SparseCore 0:
  10.0 87.0 all-gather.4
  98.9 39.7 all-gather.6
  140.6 101.0 all-gather.10
  243.4 101.1 all-gather.8
  431.8 62.1 reduce-scatter.6
  654.9 145.2 reduce-scatter.4
  803.3 180.2 reduce-scatter.8
  986.8 180.2 reduce-scatter.10
  1169.8 307.0 all-reduce.23
where the time goes:
time: 1500 us
  waiting for transfers between devices  973 us (65%)
  local copies, waits for them, and re-layouts  185 us (12%)
  matrix products  183 us (12%)
  blocking collectives  64.7 us (4%)
  starting transfers between devices  39.2 us (3%)
  other arithmetic  32.1 us (2%)
  between operations  17.8 us (1%)
    psum x1, waiting for transfers between devices, shards(): lax.psum((shard_terms[0], shard_terms[1], shard_terms[2], shard_terms[3],...  237 us
    reduce_scatter x1, waiting for transfers between devices, shards(): lax.psum_scatter(down_weight_grad, 'fsdp', scatter_dimension=1, tiled=True)  183 us
    reduce_scatter x1, waiting for transfers between devices, shards(): lax.psum_scatter(up_weight_grad, 'fsdp', scatter_dimension=0, tiled=True)  183 us
    reduce_scatter x1, waiting for transfers between devices, shards(): lax.psum_scatter(qkv_weight_grad, 'fsdp', scatter_dimension=0, tiled=True)  118 us
    all_gather x1, waiting for transfers between devices, shards(): lax.all_gather(qkv_weight, 'fsdp', axis=0, tiled=True)  61.2 us
    unnamed x2, blocking collectives  36.4 us
  transfers between devices with their start and end apart: 18, of which 14 were waited for; matrix products, arithmetic and copies ran while one was open for 21% of the time, Pallas kernels for 0%

commit v1 on v0

--- a/solution.py
+++ b/solution.py
@@ -5,6 +5,19 @@
 
 HEAD = 72
 epsilon = 1e-06
+
+
+def collect(x, axis, dim):
+    ways = lax.axis_size(axis)
+    up = [(d, (d + 1) % ways) for d in range(ways)]
+    down = [(d, (d - 1) % ways) for d in range(ways)]
+    earlier, later = ([x], [x])
+    for _ in range(ways // 2):
+        earlier.append(lax.ppermute(earlier[-1], axis, up))
+    for _ in range((ways - 1) // 2):
+        later.append(lax.ppermute(later[-1], axis, down))
+    line = jnp.concatenate([*earlier[::-1], *later[1:]], axis=dim)
+    return jnp.roll(line, (lax.axis_index(axis) - ways // 2) * x.shape[dim], axis=dim)
 
 
 def as_sent(array):
@@ -192,7 +205,7 @@
     gathered = (
         lax.all_gather(norm1_gain, "fsdp", axis=0, tiled=True),
         lax.all_gather(norm1_bias, "fsdp", axis=0, tiled=True),
-        lax.all_gather(qkv_weight, "fsdp", axis=0, tiled=True),
+        collect(qkv_weight, "fsdp", 0),
         lax.all_gather(query_bias, "fsdp", axis=0, tiled=True),
         lax.all_gather(value_bias, "fsdp", axis=0, tiled=True),
         lax.all_gather(proj_weight, "fsdp", axis=0, tiled=True),

time: 1500 us -> 1670 us (1.11)
  blocking collectives: 64.7 us -> 209 us
    unnamed x2, blocking collectives: 36.4 us -> 181 us
    ppermute x0 -> x3, waiting for transfers between devices: none -> 65.7 us  [the longest x2 65.7 us: collect(): earlier.append(lax.ppermute(earlier[-1], axis, up))]
    all_gather x1 -> x0, waiting for transfers between devices: 61.2 us -> none  [shards(): lax.all_gather(qkv_weight, 'fsdp', axis=0, tiled=True)]
    unnamed x148 -> x159, local copies, waits for them, and re-layouts: 28.7 us -> 40.9 us
  transfers between devices with their start and end apart: 18 -> 20, of which waited for: 14 -> 14; matrix products, arithmetic and copies ran while one was open for 21% -> 20% of each run, Pallas kernels for 0% -> 0%
where the time goes in v1:
time: 1670 us; the launch traced here: 1660 us
  waiting for transfers between devices  978 us (59%)
  blocking collectives  209 us (13%)
  local copies, waits for them, and re-layouts  197 us (12%)
  matrix products  182 us (11%)
  starting transfers between devices  45.6 us (3%)
  other arithmetic  31 us (2%)
  between operations  18.2 us (1%)
    psum x1, waiting for transfers between devices, shards(): lax.psum((shard_terms[0], shard_terms[1], shard_terms[2], shard_terms[3],...  237 us
    reduce_scatter x1, waiting for transfers between devices, shards(): lax.psum_scatter(down_weight_grad, 'fsdp', scatter_dimension=1, tiled=True)  183 us
    reduce_scatter x1, waiting for transfers between devices, shards(): lax.psum_scatter(up_weight_grad, 'fsdp', scatter_dimension=0, tiled=True)  183 us
    unnamed x2, blocking collectives  181 us
    reduce_scatter x1, waiting for transfers between devices, shards(): lax.psum_scatter(qkv_weight_grad, 'fsdp', scatter_dimension=0, tiled=True)  119 us
    ppermute x2, waiting for transfers between devices, collect(): earlier.append(lax.ppermute(earlier[-1], axis, up))  65.7 us
    unnamed x159, local copies, waits for them, and re-layouts  40.9 us
  transfers between devices with their start and end apart: 20, of which 14 were waited for; matrix products, arithmetic and copies ran while one was open for 20% of the time, Pallas kernels for 0%

profile of v1, /device:TPU:0, one launch (start us, length us, event | category | flops | bytes accessed | tf_op | source)
XLA Modules:
  0.0 1660.7 jit_solution(13038920929141702436)
XLA Ops:
  11.8 65.7 %collective-permute-done = bf16[288,3456]{1,0:T(8,128)(2,1)} collective-permute-done((bf16[288,3456]{1,0:T(8,128)(2,1)S(1)}, bf16[288,3456]{1,0:T(8,128)(2,1)}, u32[]{:S(2)}, u32[]{:S(2)}) %collective-permute-start) | collective-permute-done | bytes 1990688 | tf_op jit(solution)/shard_map/ppermute | solution.py:16
  85.0 163.5 %all-reduce.21 = (bf16[1152]{0:T(1024)(128)(2,1)S(1)}, bf16[1152]{0:T(1024)(128)(2,1)S(1)}, bf16[1152]{0:T(1024)(128)(2,1)S(1)}, bf16[1152]{0:T(1024)(128)(2,1)S...) all-reduce(bf16[1152]{0:T(1024)(128)(2,1)S(1)} %dynamic-update-slic, ...), channel_id=1, replica_groups=mesh['seq'=8,'fsdp'=4] {'fsdp'}, use_global_device_ids=true, to_apply=%add.1 | all-reduce | flops 13520 | bytes 54080
  280.8 26.7 %all-to-all-done = bf16[2,184,1152]{1,0,2:T(2,128)(2,1)S(1)} async-done(((bf16[2,184,1152]{1,0,2:T(2,128)(2,1)}), bf16[2,184,1152]{1,0,2:T(2,128)(2,1)S(1)}, u32[]{:S(2)}, u32[]{:S(2)}) %all-to-all-start) | async-done | bytes 847904 | tf_op jit(solution)/shard_map/all_to_all | solution.py:136
  317.7 22.7 %all-to-all-done.1 = bf16[2,184,1152]{1,0,2:T(2,128)(2,1)S(1)} async-done(((bf16[2,184,1152]{1,0,2:T(2,128)(2,1)}), bf16[2,184,1152]{1,0,2:T(2,128)(2,1)S(1)}, u32[]{:S(2)}, u32[]{:S(2)}) %all-to-all-start.1) | async-done | bytes 847904 | tf_op jit(solution)/shard_map/all_to_all | solution.py:134
  355.6 18.5 %all-to-all-done.2 = bf16[2,184,1152]{1,0,2:T(2,128)(2,1)} async-done(((bf16[2,184,1152]{1,0,2:T(2,128)(2,1)}), bf16[2,184,1152]{1,0,2:T(2,128)(2,1)}, u32[]{:S(2)}, u32[]{:S(2)}) %all-to-all-start.2) | async-done | bytes 847904 | tf_op jit(solution)/shard_map/all_to_all | solution.py:135
  383.1 30.3 %while.42 = (s32[]{:T(128)}, bf16[4,736,2,72]{1,3,2,0:T(8,128)(2,1)}, bf16[4,736,2,72]{1,3,2,0:T(8,128)(2,1)}, bf16[4,736,2,72]{1,3,2,0:T(8,128)(2,1)S(1)}, bf16...) while((s32[]{:T(128)}, bf16[4,736,2,72]{1,3,2,0:T(8,128)(2,1)}, ...), condition=%wide.region_5.6_spmd, body=%wide.region_2.5_spmd.sunk | while | flops 318626176 | bytes 9764185 | solution.py:145
  431.2 19.5 %while.43 = (s32[]{:T(128)}, bf16[4,736,2,72]{1,3,2,0:T(8,128)(2,1)}, f32[4,2,736,1]{2,1,3,0:T(2,128)S(1)}, bf16[4,736,2,72]{1,3,2,0:T(8,128)(2,1)}, bf16[4,736,...) while((s32[]{:T(128)}, ...), condition=%wide.region_11.12_spmd, body=%wide.region_8.11_spmd.sunk | while | flops 325124320 | bytes 13951333 | solution.py:145
  481.3 26.0 %all-to-all-done.4 = bf16[2,1472,144]{2,0,1:T(2,128)(2,1)} async-done(((bf16[2,1472,144]{2,0,1:T(2,128)(2,1)}), bf16[2,1472,144]{2,0,1:T(2,128)(2,1)}, u32[]{:S(2)}, u32[]{:S(2)}) %all-to-all-start.4) | async-done | bytes 847904 | tf_op jit(solution)/shard_map/all_to_all | solution.py:148
  526.5 17.5 %fusion.115 = f32[368,1152]{1,0:T(8,128)} fusion(f32[368,1152]{1,0:T(8,128)} %copy-done.23, bf16[4304,1152]{0,1:T(8,128)(2,1)} %all-gather.8.cloned.1.call-done, bf16[1152,4304]{1,0:T(8,128)(2,1)} %all-gather.6.cloned.1.call-done, f32[4304]{0:T(1024)S(1)} %convert_element_type.223, f32[1152]{0:T(1024)S(1)} %convert_element_type.225, ...), kind=kOutput, calls=%fused_computation.123 | convolution fusion | flops 7317288448 | bytes 23258304 | tf_op jit(solution)/shard_map/dot_general | solution.py:168
  566.1 9.9 multiply_reduce_fusion.4
  595.9 23.4 %all-to-all-done.5 = bf16[2,184,1152]{1,0,2:T(2,128)(2,1)} async-done(((bf16[2,184,1152]{1,0,2:T(2,128)(2,1)}), bf16[2,184,1152]{1,0,2:T(2,128)(2,1)}, u32[]{:S(2)}, u32[]{:S(2)}) %all-to-all-start.5) | async-done | bytes 847904 | tf_op jit(solution)/shard_map/all_to_all | solution.py:255
  631.3 37.4 %while.44 = (s32[]{:T(128)}, bf16[4,736,2,72]{1,3,2,0:T(8,128)(2,1)}, bf16[4,736,2,72]{1,3,2,0:T(8,128)(2,1)}, bf16[4,736,2,72]{1,3,2,0:T(8,128)(2,1)}, bf16[4,7...) while((s32[]{:T(128)}, ...), condition=%wide.region_18.19_spmd, body=%wide.region_16.18_spmd.sunk | while | flops 796823808 | bytes 38734360 | solution.py:264
  691.4 24.1 %all-to-all-done.6 = bf16[2,1472,144]{2,0,1:T(2,128)(2,1)S(1)} async-done(((bf16[2,1472,144]{2,0,1:T(2,128)(2,1)}), bf16[2,1472,144]{2,0,1:T(2,128)(2,1)S(1)}, u32[]{:S(2)}, u32[]{:S(2)}) %all-to-all-start.6) | async-done | bytes 847904 | tf_op jit(solution)/shard_map/all_to_all | solution.py:270
  732.0 24.2 %all-to-all-done.7 = bf16[2,1472,144]{2,0,1:T(2,128)(2,1)} async-done(((bf16[2,1472,144]{2,0,1:T(2,128)(2,1)}), bf16[2,1472,144]{2,0,1:T(2,128)(2,1)}, u32[]{:S(2)}, u32[]{:S(2)}) %all-to-all-start.7) | async-done | bytes 847904 | tf_op jit(solution)/shard_map/all_to_all | solution.py:273
  778.7 18.2 %all-to-all-done.8 = bf16[2,1472,144]{2,0,1:T(2,128)(2,1)} async-done(((bf16[2,1472,144]{2,0,1:T(2,128)(2,1)}), bf16[2,1472,144]{2,0,1:T(2,128)(2,1)}, u32[]{:S(2)}, u32[]{:S(2)}) %all-to-all-start.8) | async-done | bytes 847904 | tf_op jit(solution)/shard_map/all_to_all | solution.py:276
  820.6 11.5 fusion.139
  833.3 13.2 fusion.108
  846.7 118.8 %reduce-scatter.5.cloned.1.call-done = f32[288,3456]{1,0:T(8,128)} async-done(((f32[1152,3456]{1,0:T(8,128)}), f32[288,3456]{1,0:T(8,128)}) %reduce-scatter.5.cloned.1.call-update) | async-done | bytes 3981328 | tf_op jit(solution)/shard_map/reduce_scatter | solution.py:299
  965.5 183.3 %reduce-scatter.9.cloned.1.call-done = f32[288,4304]{1,0:T(8,128)} async-done(((f32[1152,4304]{1,0:T(8,128)}), f32[288,4304]{1,0:T(8,128)}) %reduce-scatter.9.cloned.1.call-update) | async-done | bytes 4958224 | tf_op jit(solution)/shard_map/reduce_scatter | solution.py:306
  1148.8 183.5 %reduce-scatter.11.cloned.1.call-done = f32[4304,288]{0,1:T(8,128)} async-done(((f32[4304,1152]{0,1:T(8,128)}), f32[4304,288]{0,1:T(8,128)}) %reduce-scatter.11.cloned.1.call-update) | async-done | bytes 4958224 | tf_op jit(solution)/shard_map/reduce_scatter | solution.py:308
  1339.9 10.7 fusion.140
  1350.6 17.2 %all-reduce.20 = (f32[1152]{0:T(1024)S(1)}, f32[1152]{0:T(1024)S(1)}, f32[1152]{0:T(1024)S(1)}, f32[1152]{0:T(1024)S(1)}, f32[1152]{0:T(1024)S(1)}, /*index=5*/f...) all-reduce(f32[1152]{0:T(1024)S(1)} %get-tuple-element.412, ...), channel_id=2, replica_groups=mesh['seq'=8,'fsdp'=4] {'fsdp'}, use_global_device_ids=true, to_apply=%region_22.23.clone | all-reduce | flops 13520 | bytes 108160
  1373.7 28.3 %all-reduce.18 = (f32[288]{0:T(512)}, f32[288]{0:T(512)}, f32[288]{0:T(512)}, f32[288]{0:T(512)}, f32[288]{0:T(512)}, /*index=5*/f32[288]{0:T(512)}, f32[288]{0:T(512)}, f32[1076]{0:T(1024)}, f32[288]{0:T(512)}) all-reduce(f32[288]{0:T(512)S(1)} %dynamic-slice.10, ...), channel_id=1, replica_groups=mesh['seq'=8,'fsdp'=4] {'seq'}, use_global_device_ids=true, to_apply=%region_23.24 | all-reduce | flops 3380 | bytes 27040 | tf_op jit(solution)/shard_map/psum | solution.py:311
  1404.9 237.1 %all-reduce.24.cloned.1.call-done = (f32[288,3456]{1,0:T(8,128)}, f32[288,1152]{1,0:T(8,128)}, f32[288,4304]{1,0:T(8,128)}, f32[4304,288]{0,1:T(8,128)}) async-done(((f32[288,3456]{1,0:T(8,128)}, f32[288,1152]{1,0:T(8,128)}, f32[288,4304]{1,0:T(8,128)}, f32[4304,288]{0,1:T(8,128)}), (f32[288,3456]{1,0:T(8,128)}, f32[288,1152]{1,0:T(8,128)}, f32[288,4304]{1,0:T(8,128)}, ...) | async-done | bytes 15224848 | tf_op jit(solution)/shard_map/psum | solution.py:311
  (375 shorter events, 398.2 us)
Async XLA Ops:
  7.3 76.9 %copy-start.50 = (bf16[288]{0:T(512)(128)(2,1)S(1)}, bf16[288]{0:T(512)(128)(2,1)}, u32[]{:S(2)}) copy-start(bf16[288]{0:T(512)(128)(2,1)} %param.34) | copy-start | bytes 1732
  7.3 77.2 %copy-start.51 = (bf16[288]{0:T(512)(128)(2,1)S(1)}, bf16[288]{0:T(512)(128)(2,1)}, u32[]{:S(2)}) copy-start(bf16[288]{0:T(512)(128)(2,1)} %param.33) | copy-start | bytes 1732
  7.3 77.4 %copy-start.42 = (bf16[1076]{0:T(1024)(128)(2,1)S(1)}, bf16[1076]{0:T(1024)(128)(2,1)}, u32[]{:S(2)}) copy-start(bf16[1076]{0:T(1024)(128)(2,1)} %param.36) | copy-start | bytes 6460
  7.3 510.3 %all-gather.4.cloned.1.call-start = ((), (), s32[]{:S(2)}) async-start(), calls=%async_computation.13 | async-start | bytes 3317760 | tf_op jit(solution)/shard_map/all_gather | solution.py:211
  8.0 518.4 %all-gather.8.cloned.1.call-start = ((), (), s32[]{:S(2)}) async-start(), calls=%async_computation.15 | async-start | bytes 12533760 | tf_op jit(solution)/shard_map/all_gather | solution.py:217
  8.8 68.8 %collective-permute-start = (bf16[288,3456]{1,0:T(8,128)(2,1)S(1)}, bf16[288,3456]{1,0:T(8,128)(2,1)}, u32[]{:S(2)}, u32[]{:S(2)}) collective-permute-start(bf16[288,3456]{1,0:T(8,128)(2,1)S(1)} %copy-done.10), channel_id=1, source_target_pairs={{0,1},{1,2},{2,3},{3,0},{4,5},{5,6},{6,7},{7,4},{8,9},{9,10},{10,1... | collective-permute-start | bytes 5971976 | tf_op jit(solution)/shard_map/ppermute | solution.py:16
  77.6 173.1 %collective-permute-start.1 = (bf16[288,3456]{1,0:T(8,128)(2,1)}, bf16[288,3456]{1,0:T(8,128)(2,1)}, u32[]{:S(2)}, u32[]{:S(2)}) collective-permute-start(bf16[288,3456]{1,0:T(8,128)(2,1)} %collective-permute-done), channel_id=1, source_target_pairs={{0,1},{1,2},{2,3},{3,0},{4,5},{5,6},{6,7},{7,4},{8,9},{9,10},{10,1... | collective-permute-start | bytes 5971976 | tf_op jit(solution)/shard_map/ppermute | solution.py:16
  78.3 176.4 %collective-permute-start.2 = (bf16[288,3456]{1,0:T(8,128)(2,1)S(1)}, bf16[288,3456]{1,0:T(8,128)(2,1)}, u32[]{:S(2)}, u32[]{:S(2)}) collective-permute-start(bf16[288,3456]{1,0:T(8,128)(2,1)S(1)} %copy-done.10), channel_id=1, source_target_pairs={{0,3},{1,0},{2,1},{3,2},{4,7},{5,4},{6,5},{7,6},{8,11},{9,8},{10,9... | collective-permute-start | bytes 5971976 | tf_op jit(solution)/shard_map/ppermute | solution.py:18
  82.7 169.9 %copy-start.36 = (f32[368]{0:T(512)}, f32[368]{0:T(512)S(1)}, u32[]{:S(2)}) copy-start(f32[368]{0:T(512)S(1)} %div.83) | copy-start | bytes 4420
  273.1 34.4 %all-to-all-start = ((bf16[2,184,1152]{1,0,2:T(2,128)(2,1)}), bf16[2,184,1152]{1,0,2:T(2,128)(2,1)S(1)}, u32[]{:S(2)}, u32[]{:S(2)}) async-start(bf16[2,184,1152]{1,0,2:T(2,128)(2,1)} %copy.166), calls=%async_computation | async-start | bytes 2359296 | tf_op jit(solution)/shard_map/all_to_all | solution.py:136
  307.5 32.9 %all-to-all-start.1 = ((bf16[2,184,1152]{1,0,2:T(2,128)(2,1)}), bf16[2,184,1152]{1,0,2:T(2,128)(2,1)S(1)}, u32[]{:S(2)}, u32[]{:S(2)}) async-start(bf16[2,184,1152]{1,0,2:T(2,128)(2,1)} %copy.169), calls=%async_computation.1 | async-start | bytes 2359296 | tf_op jit(solution)/shard_map/all_to_all | solution.py:134
  340.4 33.6 %all-to-all-start.2 = ((bf16[2,184,1152]{1,0,2:T(2,128)(2,1)}), bf16[2,184,1152]{1,0,2:T(2,128)(2,1)}, u32[]{:S(2)}, u32[]{:S(2)}) async-start(bf16[2,184,1152]{1,0,2:T(2,128)(2,1)} %copy.172), calls=%async_computation.2 | async-start | bytes 2359296 | tf_op jit(solution)/shard_map/all_to_all | solution.py:135
  344.7 181.8 %all-gather.6.cloned.1.call-start = ((), (), s32[]{:S(2)}) async-start(), calls=%async_computation.14 | async-start | bytes 12533760 | tf_op jit(solution)/shard_map/all_gather | solution.py:215
  425.6 41.1 %all-to-all-start.3 = ((bf16[2,1472,144]{2,0,1:T(2,128)(2,1)}), bf16[2,1472,144]{2,0,1:T(2,128)(2,1)}, u32[]{:S(2)}, u32[]{:S(2)}) async-start(bf16[2,1472,144]{2,0,1:T(2,128)(2,1)} %copy.179), calls=%async_computation.3 | async-start | bytes 3014656 | tf_op jit(solution)/shard_map/all_to_all | solution.py:150
  466.7 40.7 %all-to-all-start.4 = ((bf16[2,1472,144]{2,0,1:T(2,128)(2,1)}), bf16[2,1472,144]{2,0,1:T(2,128)(2,1)}, u32[]{:S(2)}, u32[]{:S(2)}) async-start(bf16[2,1472,144]{2,0,1:T(2,128)(2,1)} %copy.185), calls=%async_computation.4 | async-start | bytes 3014656 | tf_op jit(solution)/shard_map/all_to_all | solution.py:148
  585.7 33.6 %all-to-all-start.5 = ((bf16[2,184,1152]{1,0,2:T(2,128)(2,1)}), bf16[2,184,1152]{1,0,2:T(2,128)(2,1)}, u32[]{:S(2)}, u32[]{:S(2)}) async-start(bf16[2,184,1152]{1,0,2:T(2,128)(2,1)} %copy.187), calls=%async_computation.5 | async-start | bytes 2359296 | tf_op jit(solution)/shard_map/all_to_all | solution.py:255
  590.0 256.7 %reduce-scatter.7.cloned.1.call-start = ((), (), s32[]{:S(2)}) async-start(), calls=%async_computation.17 | async-start | bytes 6635520 | tf_op jit(solution)/shard_map/reduce_scatter | solution.py:302
  675.4 40.1 %all-to-all-start.6 = ((bf16[2,1472,144]{2,0,1:T(2,128)(2,1)}), bf16[2,1472,144]{2,0,1:T(2,128)(2,1)S(1)}, u32[]{:S(2)}, u32[]{:S(2)}) async-start(bf16[2,1472,144]{2,0,1:T(2,128)(2,1)} %copy.195), calls=%async_computation.6 | async-start | bytes 3014656 | tf_op jit(solution)/shard_map/all_to_all | solution.py:270
  715.5 40.7 %all-to-all-start.7 = ((bf16[2,1472,144]{2,0,1:T(2,128)(2,1)}), bf16[2,1472,144]{2,0,1:T(2,128)(2,1)}, u32[]{:S(2)}, u32[]{:S(2)}) async-start(bf16[2,1472,144]{2,0,1:T(2,128)(2,1)} %copy.198), calls=%async_computation.7 | async-start | bytes 3014656 | tf_op jit(solution)/shard_map/all_to_all | solution.py:273
  756.2 40.7 %all-to-all-start.8 = ((bf16[2,1472,144]{2,0,1:T(2,128)(2,1)}), bf16[2,1472,144]{2,0,1:T(2,128)(2,1)}, u32[]{:S(2)}, u32[]{:S(2)}) async-start(bf16[2,1472,144]{2,0,1:T(2,128)(2,1)} %copy.202), calls=%async_computation.8 | async-start | bytes 3014656 | tf_op jit(solution)/shard_map/all_to_all | solution.py:276
  760.5 205.0 %reduce-scatter.5.cloned.1.call-start = ((), (), s32[]{:S(2)}) async-start(), calls=%async_computation.16 | async-start | bytes 19906560 | tf_op jit(solution)/shard_map/reduce_scatter | solution.py:299
  819.2 329.6 %reduce-scatter.9.cloned.1.call-start = ((), (), s32[]{:S(2)}) async-start(), calls=%async_computation.18 | async-start | bytes 25067520 | tf_op jit(solution)/shard_map/reduce_scatter | solution.py:306
  832.1 500.2 %reduce-scatter.11.cloned.1.call-start = ((), (), s32[]{:S(2)}) async-start(), calls=%async_computation.19 | async-start | bytes 25067520 | tf_op jit(solution)/shard_map/reduce_scatter | solution.py:308
  846.6 795.5 %all-reduce.24.cloned.1.call-start = ((), (), s32[]{:S(2)}) async-start(), calls=%async_computation.20 | async-start | bytes 30670848 | tf_op jit(solution)/shard_map/psum | solution.py:311
  (59 other events, 965.2 us)
Sparse Core Ops, SparseCore 0:
  10.0 64.6 all-gather.3
  76.5 171.6 all-gather.7
  347.3 102.4 all-gather.5
  596.1 63.3 reduce-scatter.6
  819.3 146.1 reduce-scatter.4
  968.5 180.2 reduce-scatter.8
  1151.9 180.2 reduce-scatter.10
  1334.9 307.1 all-reduce.23
